TPU v7x, 32 devices: a whole 2x2x4 slice. The times are simulated.
32 devices in a mesh: grp: 2 (over core), row: 4 (over z), col: 4 (over y, x).
Axes of the slice: x: 2, y: 2, z: 4, core: 2. Of those that a mesh axis runs over, the one named last changes fastest.
Arguments:
- ainv_anc: bfloat16 [6144, 6144], P(('grp', 'row'), 'col'), may hold values from -12 to 12
- l_upper: bfloat16 [6144, 1024], P(('grp', 'row'), 'col'), may hold values from -0.078125 to 0.078125
- mask_upper: int32 [4, 24], replicated, may hold values from 0 to 1, as said below
- dinv_upper: float32 [256, 1024], P(None, 'col'), may hold values from -6 to 6
- l_lower: bfloat16 [6144, 1024], P(('grp', 'row'), 'col'), may hold values from -0.078125 to 0.078125
- mask_lower: int32 [4, 24], replicated, may hold values from 0 to 1, as said below
- parent: int32 [4], replicated, may hold values from 0 to 3
- lp_lower: bfloat16 [256, 1024], P(None, 'col'), may hold values from -0.375 to 0.375
- dinv_lower: float32 [256, 1024], P(None, 'col'), may hold values from -6 to 6
Outputs:
- x_upper: bfloat16 [6144, 1024], P(('grp', 'row'), 'col')
- diag_upper: bfloat16 [256, 1024], P(None, 'col')
- y_lower: bfloat16 [6144, 1024], P(('grp', 'row'), 'col')
- y_parent: bfloat16 [256, 1024], P(None, 'col')
- diag_lower: bfloat16 [256, 1024], P(None, 'col')
Inputs may be any that keep to these rules, and one draw needn't show every extreme that they name: mask_upper[u, a] is 1 where ancestor block a lies in the structure of upper supernode u. mask_lower[l, a] is 1 where ancestor block a lies in the structure of lower supernode l. parent[l] is the upper supernode whose columns hold lower supernode l's parent block.
All inputs are finite; a program needn't handle non-finite values.
Results may differ from a plain program's by a relative error of at most 0.0095.
Values may be sent and summed in bfloat16 or wider, within the bound.
A program may use at most 128 MiB of HBM per device.

v0:
```python
import jax
import jax.numpy as jnp
from jax import lax
from jax.sharding import PartitionSpec as P

B = 256


def masked_shard(factor, pattern, block_from, node_from):
    height, breadth = factor.shape
    blocks = height // B
    supernodes = breadth // B
    picked = lax.dynamic_slice(pattern, (node_from, block_from), (supernodes, blocks))
    shaped = factor.reshape(blocks, B, supernodes, B)
    keeping = (jnp.transpose(picked) > 0)[:, None, :, None]
    return jnp.where(keeping, shaped, jnp.zeros((), factor.dtype)).reshape(height, breadth)


def column_panel(masked):
    every_row = lax.all_gather(masked, ("grp", "row"), axis=0, tiled=True)
    gathered = lax.all_to_all(every_row, "col", split_axis=0, concat_axis=1, tiled=True)
    return gathered


def summed_panel(ancestor, masked):
    gathered = column_panel(masked)
    partial_value = jnp.dot(ancestor, gathered, preferred_element_type=jnp.float32)
    return lax.psum_scatter(partial_value, "col", scatter_dimension=1, tiled=True)


def on_device(
    ainv_anc, l_upper, mask_upper, dinv_upper, l_lower, mask_lower, parent, lp_lower, dinv_lower
):
    height = ainv_anc.shape[0]
    breadth = l_upper.shape[1]
    per_device = breadth // B
    block_from = lax.axis_index(("grp", "row")) * (height // B)
    node_from = lax.axis_index("col") * per_device
    upper_masked = masked_shard(l_upper, mask_upper, block_from, node_from)
    x_upper = (-summed_panel(ainv_anc, upper_masked)).astype(jnp.bfloat16)
    upper_terms = jnp.einsum(
        "akb,akc->bkc",
        upper_masked.reshape(height, per_device, B),
        x_upper.reshape(height, per_device, B),
        preferred_element_type=jnp.float32,
    ).reshape(B, breadth)
    upper_total = lax.psum(upper_terms, ("grp", "row"))
    diag_upper = (dinv_upper - upper_total).astype(jnp.bfloat16)
    lower_masked = masked_shard(l_lower, mask_lower, block_from, node_from)
    lower_sum = summed_panel(ainv_anc, lower_masked)
    x_rows, diag_rows = (
        lax.all_gather(x_upper, "col", axis=1, tiled=True),
        lax.all_gather(diag_upper, "col", axis=1, tiled=True),
    )
    parents_here = lax.dynamic_slice_in_dim(parent, node_from, per_device)
    lower_parts, crossed_parts, own_parts = ([], [], [])
    member = 0
    chosen = lax.dynamic_slice_in_dim(x_rows, parents_here[member] * B, B, 1)
    coupling = jnp.dot(chosen, lp_lower, preferred_element_type=jnp.float32)
    y_block = (-(lower_sum + coupling)).astype(jnp.bfloat16)
    lower_parts.append(y_block)
    crossed_parts.append(
        jnp.einsum("ab,ac->bc", chosen, lower_masked, preferred_element_type=jnp.float32)
    )
    own_parts.append(
        jnp.einsum("ab,ac->bc", lower_masked, y_block, preferred_element_type=jnp.float32)
    )
    y_lower = lower_parts[0]
    crossed_sum, own_sum = lax.psum((crossed_parts[0], own_parts[0]), ("grp", "row"))
    parent_parts, diag_parts = ([], [])
    member = 0
    parent_diag = lax.dynamic_slice_in_dim(diag_rows, parents_here[member] * B, B, 1)
    parent_terms = jnp.dot(parent_diag, lp_lower, preferred_element_type=jnp.float32)
    y_block = (-(crossed_sum + parent_terms)).astype(jnp.bfloat16)
    back_terms = jnp.einsum("cb,cd->bd", lp_lower, y_block, preferred_element_type=jnp.float32)
    diag_block = dinv_lower - own_sum - back_terms
    parent_parts.append(y_block)
    diag_parts.append(diag_block.astype(jnp.bfloat16))
    y_parent = parent_parts[0]
    diag_lower = diag_parts[0]
    return (x_upper, diag_upper, y_lower, y_parent, diag_lower)


def solution(mesh):
    return jax.shard_map(
        on_device,
        mesh=mesh,
        in_specs=(
            P(("grp", "row"), "col"),
            P(("grp", "row"), "col"),
            P(),
            P(None, "col"),
            P(("grp", "row"), "col"),
            P(),
            P(),
            P(None, "col"),
            P(None, "col"),
        ),
        out_specs=(
            P(("grp", "row"), "col"),
            P(None, "col"),
            P(("grp", "row"), "col"),
            P(None, "col"),
            P(None, "col"),
        ),
        check_vma=False,
    )
```

profile of v0, /device:TPU:0, one launch (start us, length us, event | category | flops | bytes accessed | tf_op | source)
XLA Modules:
  0.0 344.0 jit_solution(8300862386639493324)
XLA Ops:
  7.2 0.0 copy-start
  7.2 0.0 all-gather.4.cloned.1.call-start
  7.2 0.9 compare_bitcast_fusion
  8.2 0.1 broadcast_in_dim.28
  8.3 1.9 broadcast_select_fusion.1
  10.2 0.0 all-gather.4.cloned.1.call-update
  10.2 0.0 all-gather.6.cloned.1.call-start
  10.2 0.1 broadcast_in_dim.32
  10.3 1.9 broadcast_select_fusion
  12.3 0.0 all-gather.6.cloned.1.call-update
  12.3 0.0 reduce-scatter.3.cloned.1.call-start
  12.3 39.0 %all-gather.4.cloned.1.call-done = bf16[6144,256]{1,0:T(8,128)(2,1)} async-done(((bf16[768,256]{1,0:T(8,128)(2,1)}), bf16[6144,256]{1,0:T(8,128)(2,1)}) %all-gather.4.cloned.1.call-update) | async-done | bytes 3145744 | tf_op jit(solution)/shard_map/all_gather | solution.py:20
  51.3 42.6 %all_to_all.38 = bf16[4,1536,256]{2,1,0:T(8,128)(2,1)} all-to-all(bf16[4,1536,256]{2,1,0:T(8,128)(2,1)} %bitcast.43), channel_id=1, replica_groups=mesh['grp'=2,'row'=4,'col'=4] {'col'}, dimensions={0} | all-to-all | bytes 6291456 | tf_op jit(solution)/shard_map/all_to_all | solution.py:21
  93.9 4.6 %copy.26 = bf16[1536,4,256]{0,2,1:T(8,128)(2,1)} copy(bf16[1536,4,256]{2,0,1:T(8,128)(2,1)} %bitcast.40) | data formatting | bytes 6291456 | tf_op jit(solution)/shard_map/all_to_all | solution.py:21
  98.5 0.0 copy-done
  98.5 6.2 %convolution_bitcast_fusion.1 = f32[768,1024]{0,1:T(8,128)} fusion(bf16[1536,1024]{0,1:T(8,128)(2,1)} %bitcast.44, bf16[768,1536]{1,0:T(8,128)(2,1)S(1)} %copy-done), kind=kOutput, calls=%fused_computation.1 | convolution fusion | flops 2415919104 | bytes 8650752 | tf_op jit(solution)/shard_map/dot_general | solution.py:27
  104.7 0.0 reduce-scatter.3.cloned.1.call-update
  104.7 0.0 reduce-scatter.5.cloned.1.call-start
  104.8 0.0 all-gather.6.cloned.1.call-done
  104.8 57.3 %all_to_all.39 = bf16[4,1536,256]{2,1,0:T(8,128)(2,1)} all-to-all(bf16[4,1536,256]{2,1,0:T(8,128)(2,1)} %bitcast.42), channel_id=1, replica_groups=mesh['grp'=2,'row'=4,'col'=4] {'col'}, dimensions={0} | all-to-all | bytes 6291456 | tf_op jit(solution)/shard_map/all_to_all | solution.py:21
  162.1 4.6 %copy.28 = bf16[1536,4,256]{0,2,1:T(8,128)(2,1)} copy(bf16[1536,4,256]{2,0,1:T(8,128)(2,1)} %bitcast.41) | data formatting | bytes 6291456 | tf_op jit(solution)/shard_map/all_to_all | solution.py:21
  166.7 6.3 %convolution_bitcast_fusion = f32[768,1024]{0,1:T(8,128)} fusion(bf16[1536,1024]{0,1:T(8,128)(2,1)} %bitcast.45, bf16[768,1536]{1,0:T(8,128)(2,1)S(1)} %copy-done), kind=kOutput, calls=%fused_computation | convolution fusion | flops 2415919104 | bytes 8650752 | tf_op jit(solution)/shard_map/dot_general | solution.py:27
  173.0 0.0 copy-start.6
  173.0 0.0 copy-start.3
  173.0 0.0 copy-start.1
  173.0 0.0 reduce-scatter.5.cloned.1.call-update
  173.0 0.0 all-gather.8.cloned.1.call-start
  173.1 5.7 %reduce-scatter.3.cloned.1.call-done = f32[768,256]{0,1:T(8,128)} async-done(((f32[768,1024]{0,1:T(8,128)}), f32[768,256]{0,1:T(8,128)}) %reduce-scatter.3.cloned.1.call-update) | async-done | bytes 786448 | tf_op jit(solution)/shard_map/reduce_scatter | solution.py:28
  178.8 1.9 negate_convert_fusion
  180.7 0.0 all-gather.8.cloned.1.call-update
  180.7 0.0 copy-start.2
  180.7 0.0 all-reduce.3.cloned.1.call-start
  180.8 0.0 copy-done.6
  180.8 0.6 dynamic_slice.17
  182.0 0.0 copy-done.3
  182.1 2.0 convolution_bitcast_fusion.2
  184.0 41.5 %reduce-scatter.5.cloned.1.call-done = f32[768,256]{0,1:T(8,128)} async-done(((f32[768,1024]{0,1:T(8,128)}), f32[768,256]{0,1:T(8,128)}) %reduce-scatter.5.cloned.1.call-update) | async-done | bytes 786448 | tf_op jit(solution)/shard_map/reduce_scatter | solution.py:28
  225.6 33.1 %all-gather.8.cloned.1.call-done = bf16[768,1024]{0,1:T(8,128)(2,1)} async-done(((bf16[768,256]{0,1:T(8,128)(2,1)}), bf16[768,1024]{0,1:T(8,128)(2,1)}) %all-gather.8.cloned.1.call-update) | async-done | bytes 1572880 | tf_op jit(solution)/shard_map/all_gather | solution.py:52
  258.7 1.6 fusion.1
  260.3 0.0 copy-done.1
  260.3 1.0 fusion.13
  261.3 2.0 fusion.6
  263.3 0.0 copy-start.4
  263.3 0.0 all-reduce.3.cloned.1.call-update
  263.4 1.8 copy.27
  265.2 0.0 copy-done.2
  265.2 0.9 copy.31
  266.1 0.9 copy.33
  267.0 54.4 %all-reduce.3.cloned.1.call-done = (f32[256,256]{0,1:T(8,128)}, f32[256,256]{1,0:T(8,128)}, f32[256,256]{1,0:T(8,128)}) async-done(((f32[256,256]{0,1:T(8,128)}, f32[256,256]{1,0:T(8,128)}, f32[256,256]{1,0:T(8,128)}), (f32[256,256]{0,1:T(8,128)}, f32[256,256]{1,0:T(8,128)}, f32[256,256]{1,0:T(8,128)})) %all-reduce.3.cloned.1.call-update) | async-done | bytes 786448 | tf_op jit(solution)/shard_map/psum | solution.py:47
  321.4 1.1 subtract_convert_fusion
  322.5 0.8 copy.32
  323.3 10.7 %all_gather.15 = bf16[256,1024]{0,1:T(8,128)(2,1)S(1)} all-gather(bf16[256,256]{0,1:T(8,128)(2,1)S(1)} %subtract_convert_fusion), channel_id=1, replica_groups=mesh['grp'=2,'row'=4,'col'=4] {'col'}, dimensions={1}, use_global_device_ids=true | all-gather | bytes 655360 | tf_op jit(solution)/shard_map/all_gather | solution.py:53
  333.9 1.2 fusion.5
  335.2 0.0 copy-start.5
  335.2 0.0 copy-done.4
  335.2 2.0 fusion.4
  337.2 0.0 copy-done.5
  (2 shorter events, 0.0 us)
Async XLA Ops:
  7.2 91.4 %copy-start = (bf16[768,1536]{1,0:T(8,128)(2,1)S(1)}, bf16[768,1536]{1,0:T(8,128)(2,1)}, u32[]{:S(2)}) copy-start(bf16[768,1536]{1,0:T(8,128)(2,1)} %param.9) | copy-start | bytes 7077892
  7.2 44.1 %all-gather.4.cloned.1.call-start = ((), (), s32[]{:S(2)}) async-start(), calls=%async_computation.4 | async-start | bytes 3538944 | tf_op jit(solution)/shard_map/all_gather | solution.py:20
  10.2 94.6 %all-gather.6.cloned.1.call-start = ((), (), s32[]{:S(2)}) async-start(), calls=%async_computation.6 | async-start | bytes 3538944 | tf_op jit(solution)/shard_map/all_gather | solution.py:20
  12.3 166.5 %reduce-scatter.3.cloned.1.call-start = ((), (), s32[]{:S(2)}) async-start(), calls=%async_computation.5 | async-start | bytes 3932160 | tf_op jit(solution)/shard_map/reduce_scatter | solution.py:28
  104.7 120.8 %reduce-scatter.5.cloned.1.call-start = ((), (), s32[]{:S(2)}) async-start(), calls=%async_computation.7 | async-start | bytes 3932160 | tf_op jit(solution)/shard_map/reduce_scatter | solution.py:28
  173.0 7.8 %copy-start.6 = (s32[4]{0:T(128)S(1)}, s32[4]{0:T(128)}, u32[]{:S(2)}) copy-start(s32[4]{0:T(128)} %param.15) | copy-start | bytes 52
  173.0 9.0 %copy-start.3 = (bf16[768,256]{1,0:T(8,128)(2,1)S(1)}, bf16[768,256]{1,0:T(8,128)(2,1)}, u32[]{:S(2)}) copy-start(bf16[768,256]{1,0:T(8,128)(2,1)} %broadcast_select_fusion.1) | copy-start | bytes 1179652
  173.0 87.3 %copy-start.1 = (bf16[768,256]{1,0:T(8,128)(2,1)S(1)}, bf16[768,256]{1,0:T(8,128)(2,1)}, u32[]{:S(2)}) copy-start(bf16[768,256]{1,0:T(8,128)(2,1)} %broadcast_select_fusion) | copy-start | bytes 1179652
  173.0 85.6 %all-gather.8.cloned.1.call-start = ((), (), s32[]{:S(2)}) async-start(), calls=%async_computation.8 | async-start | bytes 1966080 | tf_op jit(solution)/shard_map/all_gather | solution.py:52
  180.7 84.5 %copy-start.2 = (bf16[768,256]{0,1:T(8,128)(2,1)S(1)}, bf16[768,256]{0,1:T(8,128)(2,1)}, u32[]{:S(2)}) copy-start(bf16[768,256]{0,1:T(8,128)(2,1)} %negate_convert_fusion) | copy-start | bytes 1179652
  180.7 140.7 %all-reduce.3.cloned.1.call-start = ((), (), s32[]{:S(2)}) async-start(), calls=%async_computation.9 | async-start | bytes 1572864 | tf_op jit(solution)/shard_map/psum | solution.py:47
  263.3 71.9 %copy-start.4 = (bf16[256,256]{1,0:T(8,128)(2,1)S(1)}, bf16[256,256]{1,0:T(8,128)(2,1)}, u32[]{:S(2)}) copy-start(bf16[256,256]{1,0:T(8,128)(2,1)} %param.16) | copy-start | bytes 393220
  335.2 2.0 copy-start.5
Sparse Core Ops, SparseCore 0:
  10.3 40.9 all-gather.3
  52.9 37.1 all-gather.5
  104.9 73.8 reduce-scatter.2
  181.6 43.8 reduce-scatter.4
  227.8 30.8 all-gather.7
  263.5 57.9 all-reduce.2
where the time goes:
time: 345 us; the launch traced here: 344 us
  waiting for transfers between devices  174 us (50%)
  blocking collectives  111 us (32%)
  matrix products  22.3 us (6%)
  between operations  14.9 us (4%)
  local copies, waits for them, and re-layouts  14.5 us (4%)
  other arithmetic  7.74 us (2%)
    all_to_all x2, blocking collectives, column_panel(): lax.all_to_all(every_row, 'col', split_axis=0, concat_axis=1, tiled=True)  99.9 us
    psum x1, waiting for transfers between devices, on_device(): upper_total = lax.psum(upper_terms, ('grp', 'row'))  54.4 us
    reduce_scatter x2, waiting for transfers between devices, summed_panel(): lax.psum_scatter(partial_value, 'col', scatter_dimension=1, tiled=True)  47.2 us
    all_gather x2, waiting for transfers between devices, column_panel(): every_row = lax.all_gather(masked, ('grp', 'row'), axis=0, tiled=True)  39 us
    all_gather x1, waiting for transfers between devices, on_device(): lax.all_gather(x_upper, 'col', axis=1, tiled=True)  33.1 us
    dot_general x2, matrix products, summed_panel(): jnp.dot(ancestor, gathered, preferred_element_type=jnp.float32)  12.5 us
    all_gather x1, blocking collectives, on_device(): lax.all_gather(diag_upper, 'col', axis=1, tiled=True)  10.7 us
    all_to_all x2, local copies, waits for them, and re-layouts, column_panel(): lax.all_to_all(every_row, 'col', split_axis=0, concat_axis=1, tiled=True)  9.26 us
  transfers between devices with their start and end apart: 6, of which 5 were waited for; matrix products, arithmetic and copies ran while one was open for 9% of the time, Pallas kernels for 0%

commit v1 on v0

v1 whole, which is shorter than its diff:
```python
import functools

import jax
import jax.numpy as jnp
from jax import lax
from jax.experimental import pallas as pl
from jax.experimental.pallas import tpu as pltpu
from jax.sharding import PartitionSpec as P

B = 256
MESH = pl.DeviceIdType.MESH
BF = jnp.bfloat16
F32 = jnp.float32


def tdot(a, b):
    return lax.dot_general(a, b, (((0,), (0,)), ((), ())), preferred_element_type=F32)


def kernel(
    G, R, C,
    a_ref, lu_ref, mu_ref, du_ref, ll_ref, ml_ref, par_ref, lp_ref, dl_ref,
    x_ref, diagu_ref, y_ref, yp_ref, diagl_ref,
    zbuf, col, part, rsb, acc, xall, rhs, lum, llm, part3, red, dufull, dpar, ypfull, ownfull,
    own_ss, z_ss, z_rs, p_ss, c_rs, r_ss, rs_ss, rs_rs, x_ss, x_rs, red_ss, red_rs,
    d_ss, d_rs, dp_ss, dp_rs, y_ss, y_rs, o_ss, o_rs,
):
    g, z, c = lax.axis_index("grp"), lax.axis_index("row"), lax.axis_index("col")
    n = G * R
    q = n // C
    r = g * R + z
    h = lu_ref.shape[0]
    hb = h // B
    S = B // n
    panels = (lu_ref, ll_ref)
    masks = (mu_ref, ml_ref)
    primary = (c * q) // R == g

    def rdev(i):
        return (lax.div(i, R), lax.rem(i, R), c)

    def copy(src, dst, ss, rs, dev):
        return pltpu.make_async_remote_copy(
            src_ref=src, dst_ref=dst, send_sem=ss, recv_sem=rs, device_id=dev, device_id_type=MESH
        )

    barrier = pltpu.get_barrier_semaphore()
    for o in range(1, n):
        pl.semaphore_signal(barrier, inc=1, device_id=rdev(lax.rem(r + o, n)), device_id_type=MESH)
    for o in range(1, C):
        pl.semaphore_signal(
            barrier, inc=1, device_id=(g, z, lax.rem(c + o, C)), device_id_type=MESH
        )
    pl.semaphore_wait(barrier, n - 1 + C - 1)

    def own_copy(p, side):
        to = z + 1 if side == 0 else z - 1
        return copy(panels[p], zbuf.at[p, z], own_ss.at[p, side], z_rs.at[p, z], (g, to, c))

    def fwd_copy(p, z0, side):
        to = z + 1 if side == 0 else z - 1
        return copy(zbuf.at[p, z0], zbuf.at[p, z0], z_ss.at[p, z0], z_rs.at[p, z0], (g, to, c))

    def plane_copy(p, z0, src):
        r0 = g * R + z0
        return copy(
            src, col.at[p, lax.rem(r0, q), c], p_ss.at[p, z0], c_rs.at[p, lax.rem(r0, q), c],
            (g, z, lax.div(r0, q)),
        )

    def relay_copy(p, j, u):
        return copy(
            col.at[p, j, u], col.at[p, j, u], r_ss.at[p, j, u], c_rs.at[p, j, u], (1 - g, z, c)
        )

    def to_plane(p, z0, src):
        r0 = g * R + z0
        d = lax.div(r0, q)

        @pl.when(d == c)
        def _():
            j = lax.rem(r0, q)
            pltpu.make_async_copy(src, col.at[p, j, c], c_rs.at[p, j, c]).start()

        @pl.when(d != c)
        def _():
            plane_copy(p, z0, src).start()

    def start_own(p):
        @pl.when(z < R - 1)
        def _():
            own_copy(p, 0).start()

        @pl.when(z > 0)
        def _():
            own_copy(p, 1).start()

        to_plane(p, z, panels[p])

    def relay(p, z0):
        r0 = g * R + z0

        @pl.when(lax.div(r0, q) == c)
        def _():
            j = lax.rem(r0, q)
            for o in range(C):
                u = lax.rem(c + o, C)
                relay_copy(p, j, u).wait_recv()
                relay_copy(p, j, u).start()

    def relay_step(p, s):
        if s == 0:
            relay(p, z)
            return

        @pl.when(z - s >= 0)
        def _():
            relay(p, z - s)

        @pl.when(z + s < R)
        def _():
            relay(p, z + s)

    def row_step(p, s):
        zl, zr = z - s, z + s

        @pl.when(zl >= 0)
        def _():
            fwd_copy(p, zl, 0).wait_recv()

            @pl.when(z < R - 1)
            def _():
                fwd_copy(p, zl, 0).start()

            to_plane(p, zl, zbuf.at[p, zl])

        @pl.when(zr < R)
        def _():
            fwd_copy(p, zr, 1).wait_recv()

            @pl.when(z > 0)
            def _():
                fwd_copy(p, zr, 1).start()

            to_plane(p, zr, zbuf.at[p, zr])

        relay_step(p, s - 1)

    def part_copy(p, o):
        u = lax.rem(c + o, C)
        return copy(part.at[p, o - 1], rsb.at[p, c], rs_ss.at[p, o], rs_rs.at[p, c], (g, z, u))

    def products(p):
        relay_step(p, R - 1)

        @pl.when(jnp.logical_not(primary))
        def _():
            for j in range(q):
                for u in range(C):
                    relay_copy(p, j, u).wait_recv()

        for o in list(range(1, C)) + [0]:
            u = lax.rem(c + o, C)

            @pl.loop(0, q * hb)
            def _(k):
                j, t = lax.div(k, hb), lax.rem(k, hb)
                keep = masks[p][u, c * q * hb + k] > 0
                rows = pl.ds(pl.multiple_of(t * B, B), B)
                blk = col[p, j, u, rows, :]
                rhs[pl.ds(pl.multiple_of(k * B, B), B), :] = jnp.where(
                    keep, blk, jnp.zeros_like(blk)
                )

            @pl.loop(0, hb)
            def _(t):
                rows = pl.ds(pl.multiple_of(t * B, B), B)
                v = jnp.dot(a_ref[rows, :], rhs[...], preferred_element_type=F32)
                if o == 0:
                    acc[p, rows, :] = v
                else:
                    part[p, o - 1, rows, :] = v.astype(BF)

            if o != 0:
                part_copy(p, o).start()

    def wait_parts(p):
        for o in range(1, C):
            s = lax.rem(c + o, C)
            copy(
                rsb.at[p, s], rsb.at[p, s], rs_ss.at[p, o], rs_rs.at[p, s], (g, z, s)
            ).wait_recv()

    def total(p, rows):
        v = acc[p, rows, :]
        for o in range(1, C):
            v = v + rsb[p, lax.rem(c + o, C), rows, :].astype(F32)
        return v

    def red_copy(k, o):
        i = lax.rem(r + o, n)
        return copy(
            part3.at[k, pl.ds(pl.multiple_of(i * S, S), S), :], red.at[k, r],
            red_ss.at[k, o], red_rs.at[k, r], rdev(i),
        )

    def send_sum(k):
        red[k, r] = part3[k, pl.ds(pl.multiple_of(r * S, S), S), :]
        for o in range(1, n):
            red_copy(k, o).start()

    def take_sum(k):
        for o in range(1, n):
            s = lax.rem(r + o, n)
            copy(
                red.at[k, s], red.at[k, s], red_ss.at[k, o], red_rs.at[k, s], rdev(s)
            ).wait_recv()
        v = red[k, 0]
        for i in range(1, n):
            v = v + red[k, i]
        return v

    mine = pl.ds(pl.multiple_of(r * S, S), S)

    def spread_copy(buf, ss, rs, o):
        return copy(buf.at[mine, :], buf.at[mine, :], ss.at[o], rs.at[r], rdev(lax.rem(r + o, n)))

    def spread(buf, ss, rs):
        for o in range(1, n):
            spread_copy(buf, ss, rs, o).start()

    def gathered(buf, ss, rs):
        for o in range(1, n):
            s = lax.rem(r + o, n)
            at = buf.at[pl.ds(pl.multiple_of(s * S, S), S), :]
            copy(at, at, ss.at[o], rs.at[s], rdev(s)).wait_recv()

    def x_copy(o):
        return copy(xall.at[c], xall.at[c], x_ss.at[o], x_rs.at[c], (g, z, lax.rem(c + o, C)))

    def dp_copy(o):
        return copy(dpar.at[c], dpar.at[c], dp_ss.at[o], dp_rs.at[c], (g, z, lax.rem(c + o, C)))

    start_own(0)

    @pl.loop(0, hb)
    def _(t):
        rows = pl.ds(pl.multiple_of(t * B, B), B)
        ub, lb = lu_ref[rows, :], ll_ref[rows, :]
        lum[rows, :] = jnp.where(mu_ref[c, r * hb + t] > 0, ub, jnp.zeros_like(ub))
        llm[rows, :] = jnp.where(ml_ref[c, r * hb + t] > 0, lb, jnp.zeros_like(lb))

    for s in range(1, R):
        row_step(0, s)
    start_own(1)
    row_step(1, 1)
    products(0)
    for s in range(2, R):
        row_step(1, s)

    wait_parts(0)

    @pl.loop(0, hb)
    def _(t):
        rows = pl.ds(pl.multiple_of(t * B, B), B)
        v = (-total(0, rows)).astype(BF)
        xall[c, rows, :] = v
        x_ref[rows, :] = v

    for o in range(1, C):
        x_copy(o).start()

    products(1)

    part3[0] = tdot(lum[...], x_ref[...])
    send_sum(0)

    for o in range(1, C):
        s = lax.rem(c + o, C)
        copy(xall.at[s], xall.at[s], x_ss.at[o], x_rs.at[s], (g, z, s)).wait_recv()
    here = par_ref[c]
    part3[1] = tdot(xall[here], llm[...])
    send_sum(1)

    dslice = (du_ref[mine, :] - take_sum(0)).astype(BF)
    dufull[mine, :] = dslice
    dpar[c] = dslice
    for o in range(1, C):
        dp_copy(o).start()
    spread(dufull, d_ss, d_rs)

    @pl.loop(0, hb)
    def _(t):
        rows = pl.ds(pl.multiple_of(t * B, B), B)
        acc[1, rows, :] += jnp.dot(xall[here, rows, :], lp_ref[...], preferred_element_type=F32)

    for o in range(1, C):
        s = lax.rem(c + o, C)
        copy(dpar.at[s], dpar.at[s], dp_ss.at[o], dp_rs.at[s], (g, z, s)).wait_recv()
    terms = jnp.dot(dpar[here], lp_ref[...], preferred_element_type=F32)
    ypfull[mine, :] = (-(take_sum(1) + terms)).astype(BF)
    spread(ypfull, y_ss, y_rs)

    wait_parts(1)

    @pl.loop(0, hb)
    def _(t):
        rows = pl.ds(pl.multiple_of(t * B, B), B)
        y_ref[rows, :] = (-total(1, rows)).astype(BF)

    part3[2] = tdot(llm[...], y_ref[...])
    send_sum(2)
    gathered(ypfull, y_ss, y_rs)
    back = tdot(lp_ref[...], ypfull[...])
    yp_ref[...] = ypfull[...]
    gathered(dufull, d_ss, d_rs)
    diagu_ref[...] = dufull[...]
    ownfull[mine, :] = take_sum(2)
    spread(ownfull, o_ss, o_rs)
    gathered(ownfull, o_ss, o_rs)
    diagl_ref[...] = (dl_ref[...] - ownfull[...] - back).astype(BF)

    for p in range(2):
        @pl.when(z < R - 1)
        def _():
            own_copy(p, 0).wait_send()

        @pl.when(z > 0)
        def _():
            own_copy(p, 1).wait_send()

        for z0 in range(R):
            @pl.when(jnp.logical_and(z0 < z, z < R - 1))
            def _():
                fwd_copy(p, z0, 0).wait_send()

            @pl.when(jnp.logical_and(z0 > z, z > 0))
            def _():
                fwd_copy(p, z0, 1).wait_send()

            @pl.when(lax.div(g * R + z0, q) != c)
            def _():
                plane_copy(p, z0, zbuf.at[p, z0]).wait_send()

        @pl.when(primary)
        def _():
            for j in range(q):
                for u in range(C):
                    relay_copy(p, j, u).wait_send()

        for o in range(1, C):
            part_copy(p, o).wait_send()
    for o in range(1, C):
        x_copy(o).wait_send()
        dp_copy(o).wait_send()
    for o in range(1, n):
        for k in range(3):
            red_copy(k, o).wait_send()
        spread_copy(dufull, d_ss, d_rs, o).wait_send()
        spread_copy(ypfull, y_ss, y_rs, o).wait_send()
        spread_copy(ownfull, o_ss, o_rs, o).wait_send()


def on_device(G, R, C, a, lu, mu, du, ll, ml, par, lp, dl):
    h = lu.shape[0]
    n = G * R
    q = n // C
    S = B // n
    vm = pl.BlockSpec(memory_space=pltpu.VMEM)
    sm = pl.BlockSpec(memory_space=pltpu.SMEM)
    dma = pltpu.SemaphoreType.DMA
    small = jax.ShapeDtypeStruct((B, B), BF)
    tall = jax.ShapeDtypeStruct((h, B), BF)
    return pl.pallas_call(
        functools.partial(kernel, G, R, C),
        out_shape=(tall, small, tall, small, small),
        in_specs=[vm, vm, sm, vm, vm, sm, sm, vm, vm],
        out_specs=(vm,) * 5,
        scratch_shapes=[
            pltpu.VMEM((2, R, h, B), BF),
            pltpu.VMEM((2, q, C, h, B), BF),
            pltpu.VMEM((2, C - 1, h, B), BF),
            pltpu.VMEM((2, C, h, B), BF),
            pltpu.VMEM((2, h, B), F32),
            pltpu.VMEM((C, h, B), BF),
            pltpu.VMEM((q * h, B), BF),
            pltpu.VMEM((h, B), BF),
            pltpu.VMEM((h, B), BF),
            pltpu.VMEM((3, B, B), F32),
            pltpu.VMEM((3, n, S, B), F32),
            pltpu.VMEM((B, B), BF),
            pltpu.VMEM((C, S, B), BF),
            pltpu.VMEM((B, B), BF),
            pltpu.VMEM((B, B), F32),
            dma((2, 2)), dma((2, R)), dma((2, R)), dma((2, R)), dma((2, q, C)), dma((2, q, C)),
            dma((2, C)), dma((2, C)), dma((C,)), dma((C,)), dma((3, n)), dma((3, n)),
            dma((n,)), dma((n,)), dma((C,)), dma((C,)), dma((n,)), dma((n,)), dma((n,)), dma((n,)),
        ],
        compiler_params=pltpu.CompilerParams(
            collective_id=0, has_side_effects=True, vmem_limit_bytes=60 * 1024 * 1024
        ),
    )(a, lu, mu, du, ll, ml, par, lp, dl)


def solution(mesh):
    tall, wide = P(("grp", "row"), "col"), P(None, "col")
    return jax.shard_map(
        functools.partial(
            on_device, mesh.shape["grp"], mesh.shape["row"], mesh.shape["col"]
        ),
        mesh=mesh,
        in_specs=(tall, tall, P(), wide, tall, P(), P(), wide, wide),
        out_specs=(tall, wide, tall, wide, wide),
        check_vma=False,
    )
```

time: 345 us -> 147 us (0.43)
  waiting for transfers between devices: 174 us -> 0 us
  Pallas kernels: 0 us -> 137 us
  blocking collectives: 111 us -> 0 us
  matrix products: 22.3 us -> 0 us
  between operations: 14.9 us -> 0.64 us
  other arithmetic: 7.74 us -> 0 us
  local copies, waits for them, and re-layouts: 14.5 us -> 8.23 us
    pallas_call x0 -> x1, Pallas kernels: none -> 137 us  [on_device(): pl.pallas_call(functools.partial(kernel, G, R, C), out_shape=(tall, small...]
    all_to_all x2 -> x0, blocking collectives: 99.9 us -> none  [column_panel(): lax.all_to_all(every_row, 'col', split_axis=0, concat_axis=1, tiled=True)]
    all_gather x3 -> x0, waiting for transfers between devices: 72.1 us -> none  [the longest x2 39 us: column_panel(): every_row = lax.all_gather(masked, ('grp', 'row'), axis=0, tiled=True)]
    psum x1 -> x0, waiting for transfers between devices: 54.4 us -> none  [on_device(): upper_total = lax.psum(upper_terms, ('grp', 'row'))]
    reduce_scatter x2 -> x0, waiting for transfers between devices: 47.2 us -> none  [summed_panel(): lax.psum_scatter(partial_value, 'col', scatter_dimension=1, tiled=True)]
    dot_general x8 -> x0, matrix products: 22.3 us -> none  [the longest x2 12.5 us: summed_panel(): jnp.dot(ancestor, gathered, preferred_element_type=jnp.float32)]
    all_gather x1 -> x0, blocking collectives: 10.7 us -> none  [on_device(): lax.all_gather(diag_upper, 'col', axis=1, tiled=True)]
    all_to_all x2 -> x0, local copies, waits for them, and re-layouts: 9.26 us -> none  [column_panel(): lax.all_to_all(every_row, 'col', split_axis=0, concat_axis=1, tiled=True)]
  transfers between devices with their start and end apart: 6 -> 0, of which waited for: 5 -> 0; matrix products, arithmetic and copies ran while one was open for 9% -> 0% of each run, Pallas kernels for 0% -> 0%
where the time goes in v1:
time: 147 us; the launch traced here: 146 us
  Pallas kernels  137 us (93%)
  local copies, waits for them, and re-layouts  8.23 us (6%)
    pallas_call x1, Pallas kernels, on_device(): pl.pallas_call(functools.partial(kernel, G, R, C), out_shape=(tall, small...  137 us
    unnamed x5, local copies, waits for them, and re-layouts  8.23 us

profile of v1, /device:TPU:0, one launch (start us, length us, event | category | flops | bytes accessed | tf_op | source)
XLA Modules:
  0.0 145.9 jit_solution(16073790343896139412)
XLA Ops:
  0.6 137.0 %shard_map.128 = (bf16[768,256]{1,0:T(8,128)(2,1)}, bf16[256,256]{1,0:T(8,128)(2,1)}, bf16[768,256]{1,0:T(8,128)(2,1)}, bf16[256,256]{1,0:T(8,128)(2,1)}, bf16[256,256]{1,0:T(8,128)(2,1)}) custom-call(bf16[768,1536]{1,0:T(8,128)(2,1)} %a_ref.1, bf16[768,256]{1,0:T(8,128)(2,1)} %lu_ref.1, s32[4,24]{1,0:T(4,128)} %mu_ref.1, f32[256,256]{1,0:T(8,128)} %du_ref.1, ...), custom_call_target="tpu_custom_call" | custom-call | tf_op jit(solution)/shard_map/pallas_call | solution.py:374
  137.7 1.8 %copy.19 = bf16[768,256]{1,0:T(8,128)(2,1)} copy(bf16[768,256]{1,0:T(8,128)(2,1)} %get-tuple-element.10) | data formatting | bytes 786432
  139.4 1.6 %copy.20 = bf16[256,256]{1,0:T(8,128)(2,1)} copy(bf16[256,256]{1,0:T(8,128)(2,1)} %get-tuple-element.11) | data formatting | bytes 262144
  141.0 1.8 %copy.21 = bf16[768,256]{1,0:T(8,128)(2,1)} copy(bf16[768,256]{1,0:T(8,128)(2,1)} %get-tuple-element.12) | data formatting | bytes 786432
  142.8 1.6 %copy.22 = bf16[256,256]{1,0:T(8,128)(2,1)} copy(bf16[256,256]{1,0:T(8,128)(2,1)} %get-tuple-element.13) | data formatting | bytes 262144
  144.3 1.6 %copy.23 = bf16[256,256]{1,0:T(8,128)(2,1)} copy(bf16[256,256]{1,0:T(8,128)(2,1)} %get-tuple-element.14) | data formatting | bytes 262144

commit v2 on v1

--- a/solution.py
+++ b/solution.py
@@ -21,20 +21,23 @@
     G, R, C,
     a_ref, lu_ref, mu_ref, du_ref, ll_ref, ml_ref, par_ref, lp_ref, dl_ref,
     x_ref, diagu_ref, y_ref, yp_ref, diagl_ref,
-    zbuf, col, part, rsb, acc, xall, rhs, lum, llm, part3, red, dufull, dpar, ypfull, ownfull,
-    own_ss, z_ss, z_rs, p_ss, c_rs, r_ss, rs_ss, rs_rs, x_ss, x_rs, red_ss, red_rs,
-    d_ss, d_rs, dp_ss, dp_rs, y_ss, y_rs, o_ss, o_rs,
+    zbuf, col, part, near, sent, last, acc, xall, rhs, lum, llm, part3, red, dufull, dpar,
+    ypfull, ownfull,
+    pre_ss, z_ss, z_rs, p_ss, c_rs, r_ss, n_ss, n_rs, l_ss, l_rs, x_ss, x_rs, xy_ss,
+    red_ss, red_rs, d_ss, d_rs, dp_ss, dp_rs, y_ss, y_rs, o_ss, o_rs,
 ):
     g, z, c = lax.axis_index("grp"), lax.axis_index("row"), lax.axis_index("col")
     n = G * R
     q = n // C
+    CX = C // G
+    y, x = lax.div(c, CX), lax.rem(c, CX)
     r = g * R + z
     h = lu_ref.shape[0]
     hb = h // B
     S = B // n
     panels = (lu_ref, ll_ref)
     masks = (mu_ref, ml_ref)
-    primary = (c * q) // R == g
+    primary = y == g
 
     def rdev(i):
         return (lax.div(i, R), lax.rem(i, R), c)
@@ -53,18 +56,23 @@
         )
     pl.semaphore_wait(barrier, n - 1 + C - 1)
 
-    def own_copy(p, side):
+    def pre_copy(p):
+        return copy(
+            panels[p], zbuf.at[p, z, y], pre_ss.at[p], z_rs.at[p, z, y], (g, z, g * CX + x)
+        )
+
+    def row_copy(p, z0, yy, side, src=None):
         to = z + 1 if side == 0 else z - 1
-        return copy(panels[p], zbuf.at[p, z], own_ss.at[p, side], z_rs.at[p, z], (g, to, c))
-
-    def fwd_copy(p, z0, side):
-        to = z + 1 if side == 0 else z - 1
-        return copy(zbuf.at[p, z0], zbuf.at[p, z0], z_ss.at[p, z0], z_rs.at[p, z0], (g, to, c))
-
-    def plane_copy(p, z0, src):
+        at = zbuf.at[p, z0, yy]
+        return copy(
+            at if src is None else src, at, z_ss.at[p, z0, yy, side], z_rs.at[p, z0, yy], (g, to, c)
+        )
+
+    def plane_copy(p, z0, yy, src):
         r0 = g * R + z0
-        return copy(
-            src, col.at[p, lax.rem(r0, q), c], p_ss.at[p, z0], c_rs.at[p, lax.rem(r0, q), c],
+        u = yy * CX + x
+        return copy(
+            src, col.at[p, lax.rem(r0, q), u], p_ss.at[p, z0, yy], c_rs.at[p, lax.rem(r0, q), u],
             (g, z, lax.div(r0, q)),
         )
 
@@ -73,29 +81,37 @@
             col.at[p, j, u], col.at[p, j, u], r_ss.at[p, j, u], c_rs.at[p, j, u], (1 - g, z, c)
         )
 
-    def to_plane(p, z0, src):
+    def to_plane(p, z0, yy, src):
         r0 = g * R + z0
         d = lax.div(r0, q)
 
         @pl.when(d == c)
         def _():
             j = lax.rem(r0, q)
-            pltpu.make_async_copy(src, col.at[p, j, c], c_rs.at[p, j, c]).start()
+            u = yy * CX + x
+            pltpu.make_async_copy(src, col.at[p, j, u], c_rs.at[p, j, u]).start()
 
         @pl.when(d != c)
         def _():
-            plane_copy(p, z0, src).start()
+            plane_copy(p, z0, yy, src).start()
+
+    def pass_on(p, z0, yy, sides, src=None):
+        if 0 in sides:
+            @pl.when(z < R - 1)
+            def _():
+                row_copy(p, z0, yy, 0, src).start()
+
+        if 1 in sides:
+            @pl.when(z > 0)
+            def _():
+                row_copy(p, z0, yy, 1, src).start()
+
+        to_plane(p, z0, yy, zbuf.at[p, z0, yy] if src is None else src)
 
     def start_own(p):
-        @pl.when(z < R - 1)
-        def _():
-            own_copy(p, 0).start()
-
-        @pl.when(z > 0)
-        def _():
-            own_copy(p, 1).start()
-
-        to_plane(p, z, panels[p])
+        pass_on(p, z, g, (0, 1), panels[p])
+        row_copy(p, z, 1 - g, 0).wait_recv()
+        pass_on(p, z, 1 - g, (0, 1))
 
     def relay(p, z0):
         r0 = g * R + z0
@@ -103,10 +119,11 @@
         @pl.when(lax.div(r0, q) == c)
         def _():
             j = lax.rem(r0, q)
-            for o in range(C):
-                u = lax.rem(c + o, C)
-                relay_copy(p, j, u).wait_recv()
-                relay_copy(p, j, u).start()
+            for o in range(CX):
+                for yy in range(G):
+                    u = yy * CX + lax.rem(x + o, CX)
+                    relay_copy(p, j, u).wait_recv()
+                    relay_copy(p, j, u).start()
 
     def relay_step(p, s):
         if s == 0:
@@ -126,32 +143,34 @@
 
         @pl.when(zl >= 0)
         def _():
-            fwd_copy(p, zl, 0).wait_recv()
-
-            @pl.when(z < R - 1)
-            def _():
-                fwd_copy(p, zl, 0).start()
-
-            to_plane(p, zl, zbuf.at[p, zl])
+            for i in range(G):
+                yy = lax.rem(g + i, G)
+                row_copy(p, zl, yy, 0).wait_recv()
+                pass_on(p, zl, yy, (0,))
 
         @pl.when(zr < R)
         def _():
-            fwd_copy(p, zr, 1).wait_recv()
-
-            @pl.when(z > 0)
-            def _():
-                fwd_copy(p, zr, 1).start()
-
-            to_plane(p, zr, zbuf.at[p, zr])
+            for i in range(G):
+                yy = lax.rem(g + i, G)
+                row_copy(p, zr, yy, 1).wait_recv()
+                pass_on(p, zr, yy, (1,))
 
         relay_step(p, s - 1)
 
-    def part_copy(p, o):
-        u = lax.rem(c + o, C)
-        return copy(part.at[p, o - 1], rsb.at[p, c], rs_ss.at[p, o], rs_rs.at[p, c], (g, z, u))
+    def near_copy(p, ux):
+        return copy(
+            part.at[p, ux], near.at[p, ux], n_ss.at[p, ux], n_rs.at[p, ux], (g, z, (1 - y) * CX + x)
+        )
+
+    def last_copy(p, ux):
+        return copy(
+            sent.at[p, ux], last.at[p, x], l_ss.at[p, ux], l_rs.at[p, x], (g, z, y * CX + ux)
+        )
 
     def products(p):
-        relay_step(p, R - 1)
+        @pl.when(primary)
+        def _():
+            relay_step(p, R - 1)
 
         @pl.when(jnp.logical_not(primary))
         def _():
@@ -159,8 +178,10 @@
                 for u in range(C):
                     relay_copy(p, j, u).wait_recv()
 
-        for o in list(range(1, C)) + [0]:
-            u = lax.rem(c + o, C)
+        offsets = list(range(1, CX)) + [0]
+        for near_side, o in [(True, o) for o in offsets] + [(False, o) for o in offsets]:
+            ux = lax.rem(x + o, CX)
+            u = ((1 - y) if near_side else y) * CX + ux
 
             @pl.loop(0, q * hb)
             def _(k):
@@ -176,25 +197,40 @@
             def _(t):
                 rows = pl.ds(pl.multiple_of(t * B, B), B)
                 v = jnp.dot(a_ref[rows, :], rhs[...], preferred_element_type=F32)
-                if o == 0:
-                    acc[p, rows, :] = v
+                if near_side:
+                    part[p, ux, rows, :] = v.astype(BF)
                 else:
-                    part[p, o - 1, rows, :] = v.astype(BF)
-
-            if o != 0:
-                part_copy(p, o).start()
+                    acc[p, ux, rows, :] = v
+
+            if near_side:
+                near_copy(p, ux).start()
+
+    def second(p):
+        for o in range(1, CX):
+            ux = lax.rem(x + o, CX)
+            near_copy(p, ux).wait_recv()
+
+            @pl.loop(0, hb)
+            def _(t):
+                rows = pl.ds(pl.multiple_of(t * B, B), B)
+                sent[p, ux, rows, :] = (
+                    acc[p, ux, rows, :] + near[p, ux, rows, :].astype(F32)
+                ).astype(BF)
+
+            last_copy(p, ux).start()
 
     def wait_parts(p):
-        for o in range(1, C):
-            s = lax.rem(c + o, C)
+        near_copy(p, x).wait_recv()
+        for o in range(1, CX):
+            ux = lax.rem(x + o, CX)
             copy(
-                rsb.at[p, s], rsb.at[p, s], rs_ss.at[p, o], rs_rs.at[p, s], (g, z, s)
+                last.at[p, ux], last.at[p, ux], l_ss.at[p, ux], l_rs.at[p, ux], (g, z, y * CX + ux)
             ).wait_recv()
 
     def total(p, rows):
-        v = acc[p, rows, :]
-        for o in range(1, C):
-            v = v + rsb[p, lax.rem(c + o, C), rows, :].astype(F32)
+        v = acc[p, x, rows, :] + near[p, x, rows, :].astype(F32)
+        for o in range(1, CX):
+            v = v + last[p, lax.rem(x + o, CX), rows, :].astype(F32)
         return v
 
     def red_copy(k, o):
@@ -236,12 +272,29 @@
             copy(at, at, ss.at[o], rs.at[s], rdev(s)).wait_recv()
 
     def x_copy(o):
-        return copy(xall.at[c], xall.at[c], x_ss.at[o], x_rs.at[c], (g, z, lax.rem(c + o, C)))
+        to = y * CX + lax.rem(x + o, CX)
+        return copy(xall.at[c], xall.at[c], x_ss.at[o], x_rs.at[c], (g, z, to))
+
+    def xy_copy(o):
+        u = y * CX + lax.rem(x + o, CX)
+        return copy(
+            xall.at[u], xall.at[u], xy_ss.at[o], x_rs.at[u], (g, z, (1 - y) * CX + x)
+        )
+
+    def wait_x(u):
+        copy(xall.at[u], xall.at[u], xy_ss.at[0], x_rs.at[u], (g, z, (1 - y) * CX + x)).wait_recv()
 
     def dp_copy(o):
         return copy(dpar.at[c], dpar.at[c], dp_ss.at[o], dp_rs.at[c], (g, z, lax.rem(c + o, C)))
 
-    start_own(0)
+    @pl.when(primary)
+    def _():
+        start_own(0)
+
+    @pl.when(jnp.logical_not(primary))
+    def _():
+        pre_copy(0).start()
+        pre_copy(1).start()
 
     @pl.loop(0, hb)
     def _(t):
@@ -250,13 +303,25 @@
         lum[rows, :] = jnp.where(mu_ref[c, r * hb + t] > 0, ub, jnp.zeros_like(ub))
         llm[rows, :] = jnp.where(ml_ref[c, r * hb + t] > 0, lb, jnp.zeros_like(lb))
 
-    for s in range(1, R):
-        row_step(0, s)
-    start_own(1)
-    row_step(1, 1)
+    @pl.when(primary)
+    def _():
+        for s in range(1, R):
+            row_step(0, s)
+        start_own(1)
+        row_step(1, 1)
+
     products(0)
-    for s in range(2, R):
-        row_step(1, s)
+
+    @pl.when(primary)
+    def _():
+        row_step(1, 2)
+
+    second(0)
+
+    @pl.when(primary)
+    def _():
+        for s in range(3, R):
+            row_step(1, s)
 
     wait_parts(0)
 
@@ -267,17 +332,20 @@
         xall[c, rows, :] = v
         x_ref[rows, :] = v
 
-    for o in range(1, C):
+    for o in range(1, CX):
         x_copy(o).start()
+    xy_copy(0).start()
 
     products(1)
 
+    for o in range(1, CX):
+        wait_x(y * CX + lax.rem(x + o, CX))
+        xy_copy(o).start()
     part3[0] = tdot(lum[...], x_ref[...])
     send_sum(0)
-
-    for o in range(1, C):
-        s = lax.rem(c + o, C)
-        copy(xall.at[s], xall.at[s], x_ss.at[o], x_rs.at[s], (g, z, s)).wait_recv()
+    second(1)
+    for o in range(CX):
+        wait_x((1 - y) * CX + lax.rem(x + o, CX))
     here = par_ref[c]
     part3[1] = tdot(xall[here], llm[...])
     send_sum(1)
@@ -292,7 +360,7 @@
     @pl.loop(0, hb)
     def _(t):
         rows = pl.ds(pl.multiple_of(t * B, B), B)
-        acc[1, rows, :] += jnp.dot(xall[here, rows, :], lp_ref[...], preferred_element_type=F32)
+        acc[1, x, rows, :] += jnp.dot(xall[here, rows, :], lp_ref[...], preferred_element_type=F32)
 
     for o in range(1, C):
         s = lax.rem(c + o, C)
@@ -321,37 +389,39 @@
     diagl_ref[...] = (dl_ref[...] - ownfull[...] - back).astype(BF)
 
     for p in range(2):
-        @pl.when(z < R - 1)
-        def _():
-            own_copy(p, 0).wait_send()
-
-        @pl.when(z > 0)
-        def _():
-            own_copy(p, 1).wait_send()
-
-        for z0 in range(R):
-            @pl.when(jnp.logical_and(z0 < z, z < R - 1))
-            def _():
-                fwd_copy(p, z0, 0).wait_send()
-
-            @pl.when(jnp.logical_and(z0 > z, z > 0))
-            def _():
-                fwd_copy(p, z0, 1).wait_send()
-
-            @pl.when(lax.div(g * R + z0, q) != c)
-            def _():
-                plane_copy(p, z0, zbuf.at[p, z0]).wait_send()
-
         @pl.when(primary)
         def _():
+            for z0 in range(R):
+                for yy in range(G):
+                    @pl.when(jnp.logical_and(z0 <= z, z < R - 1))
+                    def _():
+                        row_copy(p, z0, yy, 0).wait_send()
+
+                    @pl.when(jnp.logical_and(z0 >= z, z > 0))
+                    def _():
+                        row_copy(p, z0, yy, 1).wait_send()
+
+                    @pl.when(lax.div(g * R + z0, q) != c)
+                    def _():
+                        plane_copy(p, z0, yy, zbuf.at[p, z0, yy]).wait_send()
+
             for j in range(q):
                 for u in range(C):
                     relay_copy(p, j, u).wait_send()
 
-        for o in range(1, C):
-            part_copy(p, o).wait_send()
+        @pl.when(jnp.logical_not(primary))
+        def _():
+            pre_copy(p).wait_send()
+
+        for ux in range(CX):
+            near_copy(p, ux).wait_send()
+        for o in range(1, CX):
+            last_copy(p, lax.rem(x + o, CX)).wait_send()
+    for o in range(CX):
+        xy_copy(o).wait_send()
+    for o in range(1, CX):
+        x_copy(o).wait_send()
     for o in range(1, C):
-        x_copy(o).wait_send()
         dp_copy(o).wait_send()
     for o in range(1, n):
         for k in range(3):
@@ -366,6 +436,7 @@
     n = G * R
     q = n // C
     S = B // n
+    CX = C // G
     vm = pl.BlockSpec(memory_space=pltpu.VMEM)
     sm = pl.BlockSpec(memory_space=pltpu.SMEM)
     dma = pltpu.SemaphoreType.DMA
@@ -377,11 +448,13 @@
         in_specs=[vm, vm, sm, vm, vm, sm, sm, vm, vm],
         out_specs=(vm,) * 5,
         scratch_shapes=[
-            pltpu.VMEM((2, R, h, B), BF),
+            pltpu.VMEM((2, R, G, h, B), BF),
             pltpu.VMEM((2, q, C, h, B), BF),
-            pltpu.VMEM((2, C - 1, h, B), BF),
-            pltpu.VMEM((2, C, h, B), BF),
-            pltpu.VMEM((2, h, B), F32),
+            pltpu.VMEM((2, CX, h, B), BF),
+            pltpu.VMEM((2, CX, h, B), BF),
+            pltpu.VMEM((2, CX, h, B), BF),
+            pltpu.VMEM((2, CX, h, B), BF),
+            pltpu.VMEM((2, CX, h, B), F32),
             pltpu.VMEM((C, h, B), BF),
             pltpu.VMEM((q * h, B), BF),
             pltpu.VMEM((h, B), BF),
@@ -392,8 +465,9 @@
             pltpu.VMEM((C, S, B), BF),
             pltpu.VMEM((B, B), BF),
             pltpu.VMEM((B, B), F32),
-            dma((2, 2)), dma((2, R)), dma((2, R)), dma((2, R)), dma((2, q, C)), dma((2, q, C)),
-            dma((2, C)), dma((2, C)), dma((C,)), dma((C,)), dma((3, n)), dma((3, n)),
+            dma((2,)), dma((2, R, G, 2)), dma((2, R, G)), dma((2, R, G)), dma((2, q, C)),
+            dma((2, q, C)), dma((2, CX)), dma((2, CX)), dma((2, CX)), dma((2, CX)),
+            dma((CX,)), dma((C,)), dma((CX,)), dma((3, n)), dma((3, n)),
             dma((n,)), dma((n,)), dma((C,)), dma((C,)), dma((n,)), dma((n,)), dma((n,)), dma((n,)),
         ],
         compiler_params=pltpu.CompilerParams(

time: 147 us -> 150 us (1.020); the launches traced: 146 us -> 147 us
  no operation moved by 1% of the time
where the time goes in v2:
time: 150 us; the launch traced here: 147 us
  Pallas kernels  138 us (92%)
  local copies, waits for them, and re-layouts  8.23 us (5%)
    pallas_call x1, Pallas kernels, on_device(): pl.pallas_call(functools.partial(kernel, G, R, C), out_shape=(tall, small...  138 us
    unnamed x5, local copies, waits for them, and re-layouts  8.23 us

profile of v2, /device:TPU:0, one launch (start us, length us, event | category | flops | bytes accessed | tf_op | source)
XLA Modules:
  0.0 147.0 jit_solution(8977631123256041946)
XLA Ops:
  0.6 138.1 %shard_map.128 = (bf16[768,256]{1,0:T(8,128)(2,1)}, bf16[256,256]{1,0:T(8,128)(2,1)}, bf16[768,256]{1,0:T(8,128)(2,1)}, bf16[256,256]{1,0:T(8,128)(2,1)}, bf16[256,256]{1,0:T(8,128)(2,1)}) custom-call(bf16[768,1536]{1,0:T(8,128)(2,1)} %a_ref.1, bf16[768,256]{1,0:T(8,128)(2,1)} %lu_ref.1, s32[4,24]{1,0:T(4,128)} %mu_ref.1, f32[256,256]{1,0:T(8,128)} %du_ref.1, ...), custom_call_target="tpu_custom_call" | custom-call | tf_op jit(solution)/shard_map/pallas_call | solution.py:445
  138.8 1.8 %copy.19 = bf16[768,256]{1,0:T(8,128)(2,1)} copy(bf16[768,256]{1,0:T(8,128)(2,1)} %get-tuple-element.10) | data formatting | bytes 786432
  140.5 1.6 %copy.20 = bf16[256,256]{1,0:T(8,128)(2,1)} copy(bf16[256,256]{1,0:T(8,128)(2,1)} %get-tuple-element.11) | data formatting | bytes 262144
  142.1 1.8 %copy.21 = bf16[768,256]{1,0:T(8,128)(2,1)} copy(bf16[768,256]{1,0:T(8,128)(2,1)} %get-tuple-element.12) | data formatting | bytes 786432
  143.9 1.6 %copy.22 = bf16[256,256]{1,0:T(8,128)(2,1)} copy(bf16[256,256]{1,0:T(8,128)(2,1)} %get-tuple-element.13) | data formatting | bytes 262144
  145.4 1.6 %copy.23 = bf16[256,256]{1,0:T(8,128)(2,1)} copy(bf16[256,256]{1,0:T(8,128)(2,1)} %get-tuple-element.14) | data formatting | bytes 262144

commit v3 on v2

--- a/solution.py
+++ b/solution.py
@@ -9,6 +9,7 @@
 
 B = 256
 MESH = pl.DeviceIdType.MESH
+W = 2
 BF = jnp.bfloat16
 F32 = jnp.float32
 
@@ -56,32 +57,40 @@
         )
     pl.semaphore_wait(barrier, n - 1 + C - 1)
 
-    def pre_copy(p):
-        return copy(
-            panels[p], zbuf.at[p, z, y], pre_ss.at[p], z_rs.at[p, z, y], (g, z, g * CX + x)
-        )
-
-    def row_copy(p, z0, yy, side, src=None):
+    def cutr(w):
+        return pl.ds(w * (h // W), h // W)
+
+    def pre_copy(p, w):
+        return copy(
+            panels[p].at[cutr(w), :], zbuf.at[p, z, y, cutr(w), :], pre_ss.at[p, w],
+            z_rs.at[p, z, y, w], (g, z, g * CX + x),
+        )
+
+    def row_copy(p, z0, yy, side, w, own=False):
         to = z + 1 if side == 0 else z - 1
-        at = zbuf.at[p, z0, yy]
-        return copy(
-            at if src is None else src, at, z_ss.at[p, z0, yy, side], z_rs.at[p, z0, yy], (g, to, c)
-        )
-
-    def plane_copy(p, z0, yy, src):
+        at = zbuf.at[p, z0, yy, cutr(w), :]
+        return copy(
+            panels[p].at[cutr(w), :] if own else at, at, z_ss.at[p, z0, yy, side, w],
+            z_rs.at[p, z0, yy, w], (g, to, c),
+        )
+
+    def piece(p, z0, yy, w, own):
+        return panels[p].at[cutr(w), :] if own else zbuf.at[p, z0, yy, cutr(w), :]
+
+    def plane_copy(p, z0, yy, w, own=False):
         r0 = g * R + z0
         u = yy * CX + x
-        return copy(
-            src, col.at[p, lax.rem(r0, q), u], p_ss.at[p, z0, yy], c_rs.at[p, lax.rem(r0, q), u],
-            (g, z, lax.div(r0, q)),
-        )
-
-    def relay_copy(p, j, u):
-        return copy(
-            col.at[p, j, u], col.at[p, j, u], r_ss.at[p, j, u], c_rs.at[p, j, u], (1 - g, z, c)
-        )
-
-    def to_plane(p, z0, yy, src):
+        j = lax.rem(r0, q)
+        return copy(
+            piece(p, z0, yy, w, own), col.at[p, j, u, cutr(w), :], p_ss.at[p, z0, yy, w],
+            c_rs.at[p, j, u, w], (g, z, lax.div(r0, q)),
+        )
+
+    def relay_copy(p, j, u, w):
+        at = col.at[p, j, u, cutr(w), :]
+        return copy(at, at, r_ss.at[p, j, u, w], c_rs.at[p, j, u, w], (1 - g, z, c))
+
+    def to_plane(p, z0, yy, w, own):
         r0 = g * R + z0
         d = lax.div(r0, q)
 
@@ -89,29 +98,33 @@
         def _():
             j = lax.rem(r0, q)
             u = yy * CX + x
-            pltpu.make_async_copy(src, col.at[p, j, u], c_rs.at[p, j, u]).start()
+            pltpu.make_async_copy(
+                piece(p, z0, yy, w, own), col.at[p, j, u, cutr(w), :], c_rs.at[p, j, u, w]
+            ).start()
 
         @pl.when(d != c)
         def _():
-            plane_copy(p, z0, yy, src).start()
-
-    def pass_on(p, z0, yy, sides, src=None):
+            plane_copy(p, z0, yy, w, own).start()
+
+    def pass_on(p, z0, yy, sides, w, own=False):
         if 0 in sides:
             @pl.when(z < R - 1)
             def _():
-                row_copy(p, z0, yy, 0, src).start()
+                row_copy(p, z0, yy, 0, w, own).start()
 
         if 1 in sides:
             @pl.when(z > 0)
             def _():
-                row_copy(p, z0, yy, 1, src).start()
-
-        to_plane(p, z0, yy, zbuf.at[p, z0, yy] if src is None else src)
+                row_copy(p, z0, yy, 1, w, own).start()
+
+        to_plane(p, z0, yy, w, own)
 
     def start_own(p):
-        pass_on(p, z, g, (0, 1), panels[p])
-        row_copy(p, z, 1 - g, 0).wait_recv()
-        pass_on(p, z, 1 - g, (0, 1))
+        for w in range(W):
+            pass_on(p, z, g, (0, 1), w, True)
+        for w in range(W):
+            row_copy(p, z, 1 - g, 0, w).wait_recv()
+            pass_on(p, z, 1 - g, (0, 1), w)
 
     def relay(p, z0):
         r0 = g * R + z0
@@ -121,11 +134,14 @@
             j = lax.rem(r0, q)
             for o in range(CX):
                 for yy in range(G):
-                    u = yy * CX + lax.rem(x + o, CX)
-                    relay_copy(p, j, u).wait_recv()
-                    relay_copy(p, j, u).start()
+                    for w in range(W):
+                        u = yy * CX + lax.rem(x + o, CX)
+                        relay_copy(p, j, u, w).wait_recv()
+                        relay_copy(p, j, u, w).start()
 
     def relay_step(p, s):
+        if s < 0:
+            return
         if s == 0:
             relay(p, z)
             return
@@ -140,22 +156,21 @@
 
     def row_step(p, s):
         zl, zr = z - s, z + s
-
-        @pl.when(zl >= 0)
-        def _():
-            for i in range(G):
+        for i in range(G):
+            for w in range(W):
                 yy = lax.rem(g + i, G)
-                row_copy(p, zl, yy, 0).wait_recv()
-                pass_on(p, zl, yy, (0,))
-
-        @pl.when(zr < R)
-        def _():
-            for i in range(G):
-                yy = lax.rem(g + i, G)
-                row_copy(p, zr, yy, 1).wait_recv()
-                pass_on(p, zr, yy, (1,))
-
-        relay_step(p, s - 1)
+
+                @pl.when(zl >= 0)
+                def _():
+                    row_copy(p, zl, yy, 0, w).wait_recv()
+                    pass_on(p, zl, yy, (0,), w)
+
+                @pl.when(zr < R)
+                def _():
+                    row_copy(p, zr, yy, 1, w).wait_recv()
+                    pass_on(p, zr, yy, (1,), w)
+
+        relay_step(p, s - 2)
 
     def near_copy(p, ux):
         return copy(
@@ -170,13 +185,15 @@
     def products(p):
         @pl.when(primary)
         def _():
-            relay_step(p, R - 1)
+            for s in range(max(R - 2, 0), R):
+                relay_step(p, s)
 
         @pl.when(jnp.logical_not(primary))
         def _():
             for j in range(q):
                 for u in range(C):
-                    relay_copy(p, j, u).wait_recv()
+                    for w in range(W):
+                        relay_copy(p, j, u, w).wait_recv()
 
         offsets = list(range(1, CX)) + [0]
         for near_side, o in [(True, o) for o in offsets] + [(False, o) for o in offsets]:
@@ -271,18 +288,20 @@
             at = buf.at[pl.ds(pl.multiple_of(s * S, S), S), :]
             copy(at, at, ss.at[o], rs.at[s], rdev(s)).wait_recv()
 
-    def x_copy(o):
-        to = y * CX + lax.rem(x + o, CX)
-        return copy(xall.at[c], xall.at[c], x_ss.at[o], x_rs.at[c], (g, z, to))
-
-    def xy_copy(o):
-        u = y * CX + lax.rem(x + o, CX)
-        return copy(
-            xall.at[u], xall.at[u], xy_ss.at[o], x_rs.at[u], (g, z, (1 - y) * CX + x)
+    def xn_copy():
+        return copy(
+            xall.at[c], xall.at[c], x_ss.at[0], x_rs.at[c], (g, z, (1 - y) * CX + x)
+        )
+
+    def xr_copy(o, yy):
+        u = yy * CX + x
+        return copy(
+            xall.at[u], xall.at[u], xy_ss.at[o, yy], x_rs.at[u],
+            (g, z, y * CX + lax.rem(x + o, CX)),
         )
 
     def wait_x(u):
-        copy(xall.at[u], xall.at[u], xy_ss.at[0], x_rs.at[u], (g, z, (1 - y) * CX + x)).wait_recv()
+        copy(xall.at[u], xall.at[u], x_ss.at[0], x_rs.at[u], (g, z, (1 - y) * CX + x)).wait_recv()
 
     def dp_copy(o):
         return copy(dpar.at[c], dpar.at[c], dp_ss.at[o], dp_rs.at[c], (g, z, lax.rem(c + o, C)))
@@ -293,8 +312,9 @@
 
     @pl.when(jnp.logical_not(primary))
     def _():
-        pre_copy(0).start()
-        pre_copy(1).start()
+        for p in range(2):
+            for w in range(W):
+                pre_copy(p, w).start()
 
     @pl.loop(0, hb)
     def _(t):
@@ -332,20 +352,21 @@
         xall[c, rows, :] = v
         x_ref[rows, :] = v
 
+    xn_copy().start()
     for o in range(1, CX):
-        x_copy(o).start()
-    xy_copy(0).start()
+        xr_copy(o, y).start()
 
     products(1)
 
+    wait_x((1 - y) * CX + x)
     for o in range(1, CX):
-        wait_x(y * CX + lax.rem(x + o, CX))
-        xy_copy(o).start()
+        xr_copy(o, 1 - y).start()
     part3[0] = tdot(lum[...], x_ref[...])
     send_sum(0)
     second(1)
-    for o in range(CX):
-        wait_x((1 - y) * CX + lax.rem(x + o, CX))
+    for o in range(1, CX):
+        for yy in range(G):
+            wait_x(yy * CX + lax.rem(x + o, CX))
     here = par_ref[c]
     part3[1] = tdot(xall[here], llm[...])
     send_sum(1)
@@ -393,34 +414,37 @@
         def _():
             for z0 in range(R):
                 for yy in range(G):
-                    @pl.when(jnp.logical_and(z0 <= z, z < R - 1))
-                    def _():
-                        row_copy(p, z0, yy, 0).wait_send()
-
-                    @pl.when(jnp.logical_and(z0 >= z, z > 0))
-                    def _():
-                        row_copy(p, z0, yy, 1).wait_send()
-
-                    @pl.when(lax.div(g * R + z0, q) != c)
-                    def _():
-                        plane_copy(p, z0, yy, zbuf.at[p, z0, yy]).wait_send()
+                    for w in range(W):
+                        @pl.when(jnp.logical_and(z0 <= z, z < R - 1))
+                        def _():
+                            row_copy(p, z0, yy, 0, w).wait_send()
+
+                        @pl.when(jnp.logical_and(z0 >= z, z > 0))
+                        def _():
+                            row_copy(p, z0, yy, 1, w).wait_send()
+
+                        @pl.when(lax.div(g * R + z0, q) != c)
+                        def _():
+                            plane_copy(p, z0, yy, w).wait_send()
 
             for j in range(q):
                 for u in range(C):
-                    relay_copy(p, j, u).wait_send()
+                    for w in range(W):
+                        relay_copy(p, j, u, w).wait_send()
 
         @pl.when(jnp.logical_not(primary))
         def _():
-            pre_copy(p).wait_send()
+            for w in range(W):
+                pre_copy(p, w).wait_send()
 
         for ux in range(CX):
             near_copy(p, ux).wait_send()
         for o in range(1, CX):
             last_copy(p, lax.rem(x + o, CX)).wait_send()
-    for o in range(CX):
-        xy_copy(o).wait_send()
+    xn_copy().wait_send()
     for o in range(1, CX):
-        x_copy(o).wait_send()
+        for yy in range(G):
+            xr_copy(o, yy).wait_send()
     for o in range(1, C):
         dp_copy(o).wait_send()
     for o in range(1, n):
@@ -465,9 +489,9 @@
             pltpu.VMEM((C, S, B), BF),
             pltpu.VMEM((B, B), BF),
             pltpu.VMEM((B, B), F32),
-            dma((2,)), dma((2, R, G, 2)), dma((2, R, G)), dma((2, R, G)), dma((2, q, C)),
-            dma((2, q, C)), dma((2, CX)), dma((2, CX)), dma((2, CX)), dma((2, CX)),
-            dma((CX,)), dma((C,)), dma((CX,)), dma((3, n)), dma((3, n)),
+            dma((2, W)), dma((2, R, G, 2, W)), dma((2, R, G, W)), dma((2, R, G, W)),
+            dma((2, q, C, W)), dma((2, q, C, W)), dma((2, CX)), dma((2, CX)), dma((2, CX)), dma((2, CX)),
+            dma((1,)), dma((C,)), dma((CX, G)), dma((3, n)), dma((3, n)),
             dma((n,)), dma((n,)), dma((C,)), dma((C,)), dma((n,)), dma((n,)), dma((n,)), dma((n,)),
         ],
         compiler_params=pltpu.CompilerParams(

time: 150 us -> 138 us (0.920); the launches traced: 147 us -> 137 us
  Pallas kernels: 138 us -> 128 us
    pallas_call x1, Pallas kernels: 138 us -> 128 us  [on_device(): pl.pallas_call(functools.partial(kernel, G, R, C), out_shape=(tall, small...]
where the time goes in v3:
time: 138 us; the launch traced here: 137 us
  Pallas kernels  128 us (93%)
  local copies, waits for them, and re-layouts  8.23 us (6%)
    pallas_call x1, Pallas kernels, on_device(): pl.pallas_call(functools.partial(kernel, G, R, C), out_shape=(tall, small...  128 us
    unnamed x5, local copies, waits for them, and re-layouts  8.23 us

profile of v3, /device:TPU:0, one launch (start us, length us, event | category | flops | bytes accessed | tf_op | source)
XLA Modules:
  0.0 137.2 jit_solution(3774005264176668840)
XLA Ops:
  0.6 128.4 %shard_map.128 = (bf16[768,256]{1,0:T(8,128)(2,1)}, bf16[256,256]{1,0:T(8,128)(2,1)}, bf16[768,256]{1,0:T(8,128)(2,1)}, bf16[256,256]{1,0:T(8,128)(2,1)}, bf16[256,256]{1,0:T(8,128)(2,1)}) custom-call(bf16[768,1536]{1,0:T(8,128)(2,1)} %a_ref.1, bf16[768,256]{1,0:T(8,128)(2,1)} %lu_ref.1, s32[4,24]{1,0:T(4,128)} %mu_ref.1, f32[256,256]{1,0:T(8,128)} %du_ref.1, ...), custom_call_target="tpu_custom_call" | custom-call | tf_op jit(solution)/shard_map/pallas_call | solution.py:469
  129.0 1.8 %copy.19 = bf16[768,256]{1,0:T(8,128)(2,1)} copy(bf16[768,256]{1,0:T(8,128)(2,1)} %get-tuple-element.10) | data formatting | bytes 786432
  130.8 1.6 %copy.20 = bf16[256,256]{1,0:T(8,128)(2,1)} copy(bf16[256,256]{1,0:T(8,128)(2,1)} %get-tuple-element.11) | data formatting | bytes 262144
  132.3 1.8 %copy.21 = bf16[768,256]{1,0:T(8,128)(2,1)} copy(bf16[768,256]{1,0:T(8,128)(2,1)} %get-tuple-element.12) | data formatting | bytes 786432
  134.1 1.6 %copy.22 = bf16[256,256]{1,0:T(8,128)(2,1)} copy(bf16[256,256]{1,0:T(8,128)(2,1)} %get-tuple-element.13) | data formatting | bytes 262144
  135.7 1.6 %copy.23 = bf16[256,256]{1,0:T(8,128)(2,1)} copy(bf16[256,256]{1,0:T(8,128)(2,1)} %get-tuple-element.14) | data formatting | bytes 262144
